TPU v7x, 32 devices: a whole 2x2x4 slice. The times are simulated.
32 devices in a mesh: far: 4 (over z), near: 8 (over y, x, core).
Axes of the slice: x: 2, y: 2, z: 4, core: 2. Of those that a mesh axis runs over, the one named last changes fastest.
Arguments:
- state_real: float32 [4, 8, 2, 128, 128], P('far', 'near'), may hold values from -5 to 5
- state_imag: float32 [4, 8, 2, 128, 128], P('far', 'near'), may hold values from -5 to 5
- gate_real: float32 [2, 4, 3, 128, 128], replicated, may hold values from -0.375 to 0.375
- gate_imag: float32 [2, 4, 3, 128, 128], replicated, may hold values from -0.375 to 0.375
Outputs:
- final_real: float32 [4, 8, 2, 128, 128], P('far', 'near')
- final_imag: float32 [4, 8, 2, 128, 128], P('far', 'near')
All inputs are finite; a program needn't handle non-finite values.
Results may differ from a plain program's by a relative error of at most 0.000071.
Values sent between devices are 32-bit elements; how exact they have to be, the bound alone decides.
A program may use at most 64 MiB of HBM per device.

v0:
```python
import jax
import jax.numpy as jnp
from jax import lax
from jax.sharding import PartitionSpec as P


def gate_low(x, g):
    return jnp.einsum(
        "...l,jl->...j", x, g, precision=lax.Precision.HIGHEST, preferred_element_type=jnp.float32
    )


def gate_mid(x, g):
    return jnp.einsum(
        "...ml,jm->...jl", x, g, precision=lax.Precision.HIGHEST, preferred_element_type=jnp.float32
    )


def gate_top(x, g):
    high, width, lows = (x.shape[-3], x.shape[-2], x.shape[-1])
    upper = g.shape[0] // high
    lead = x.shape[:-3]
    viewed = x.reshape(lead + (high, upper, width // upper, lows))
    matrix = g.reshape((g.shape[0], high, upper))
    out = jnp.einsum(
        "...hkrl,jhk->...jrl",
        viewed,
        matrix,
        precision=lax.Precision.HIGHEST,
        preferred_element_type=jnp.float32,
    )
    return out.reshape(lead + (high, width, lows))


def complex_gate(form, real, imag, greal, gimag):
    new_real = form(real, greal) - form(imag, gimag)
    new_imag = form(imag, greal) + form(real, gimag)
    return (new_real, new_imag)


def merged_rows(x):
    return x.reshape((1, 1, x.shape[2] * x.shape[3], x.shape[4]))


def on_device(state_real, state_imag, gate_real, gate_imag):
    real, imag = (state_real, state_imag)
    forms = (gate_low, gate_mid, gate_top)
    shape = state_real.shape
    for rnd in range(gate_real.shape[0]):
        for section in range(4):
            if section == 2:
                order = [1, 0, 2]
            else:
                order = [0, 1, 2]
            early = []
            later = order[len(early) :]
            pair = (real, imag)
            if section == 0:
                moved = (
                    lax.all_to_all(
                        merged_rows(pair[0]), "far", split_axis=2, concat_axis=2, tiled=True
                    ),
                    lax.all_to_all(
                        merged_rows(pair[1]), "far", split_axis=2, concat_axis=2, tiled=True
                    ),
                )
                pair = (moved[0].reshape(shape), moved[1].reshape(shape))
            elif section == 1:
                pair = (
                    lax.all_to_all(pair[0], "near", split_axis=3, concat_axis=3, tiled=True),
                    lax.all_to_all(pair[1], "near", split_axis=3, concat_axis=3, tiled=True),
                )
            elif section == 2:
                pair = (
                    lax.all_to_all(pair[0], "near", split_axis=4, concat_axis=4, tiled=True),
                    lax.all_to_all(pair[1], "near", split_axis=4, concat_axis=4, tiled=True),
                )
            else:
                moved = (
                    lax.all_to_all(
                        merged_rows(pair[0]), "near", split_axis=2, concat_axis=2, tiled=True
                    ),
                    lax.all_to_all(
                        merged_rows(pair[1]), "near", split_axis=2, concat_axis=2, tiled=True
                    ),
                )
                pair = (moved[0].reshape(shape), moved[1].reshape(shape))
            for which in later:
                pair = complex_gate(
                    forms[which],
                    pair[0],
                    pair[1],
                    gate_real[rnd, section, which],
                    gate_imag[rnd, section, which],
                )
            real, imag = pair
    return (real, imag)


def solution(mesh):
    return jax.shard_map(
        on_device,
        mesh=mesh,
        in_specs=(P("far", "near", None, None, None), P("far", "near", None, None, None), P(), P()),
        out_specs=(P("far", "near", None, None, None), P("far", "near", None, None, None)),
        check_vma=False,
    )
```

profile of v0, /device:TPU:0, one launch (start us, length us, event | category | flops | bytes accessed | tf_op | source)
XLA Modules:
  0.0 206.7 jit_solution(93294807421367379)
XLA Ops:
  0.6 6.5 %all-to-all-start.1 = ((f32[1,1,256,128]{3,1,0,2:T(1,128)}), f32[1,1,256,128]{3,1,0,2:T(1,128)S(1)}, u32[]{:S(2)}, u32[]{:S(2)}) async-start(f32[1,1,256,128]{3,1,0,2:T(1,128)} %bitcast.836), calls=%async_computation.1 | async-start | bytes 262144 | tf_op jit(solution)/shard_map/all_to_all | solution.py:63
  7.1 1.7 fusion.261
  10.3 1.7 copy.198
  12.0 1.6 copy.186
  17.5 1.6 copy.216
  19.1 1.6 copy.200
  20.6 1.6 copy.188
  22.2 1.6 copy.178
  23.7 1.6 copy.168
  26.7 5.1 %all-to-all-start = ((f32[1,1,256,128]{3,1,0,2:T(1,128)}), f32[1,1,256,128]{3,1,0,2:T(1,128)S(1)}, u32[]{:S(2)}, u32[]{:S(2)}) async-start(f32[1,1,256,128]{3,1,0,2:T(1,128)} %bitcast.837), calls=%async_computation | async-start | bytes 262144 | tf_op jit(solution)/shard_map/all_to_all | solution.py:60
  32.8 5.0 %all-to-all-done = f32[1,1,256,128]{3,1,0,2:T(1,128)S(1)} async-done(((f32[1,1,256,128]{3,1,0,2:T(1,128)}), f32[1,1,256,128]{3,1,0,2:T(1,128)S(1)}, u32[]{:S(2)}, u32[]{:S(2)}) %all-to-all-start) | async-done | bytes 131104 | tf_op jit(solution)/shard_map/all_to_all | solution.py:60
  38.1 1.2 convolution_add_fusion.15
  43.2 3.7 %all-to-all-start.3 = ((f32[1,1,2,128,128]{4,2,1,0,3:T(2,128)}), f32[1,1,2,128,128]{4,2,1,0,3:T(2,128)S(1)}, u32[]{:S(2)}, u32[]{:S(2)}) async-start(f32[1,1,2,128,128]{4,2,1,0,3:T(2,128)} %copy.148), calls=%async_computation.3 | async-start | bytes 262144 | tf_op jit(solution)/shard_map/all_to_all | solution.py:71
  46.9 1.3 fusion.35
  49.0 3.4 %all-to-all-done.3 = f32[1,1,2,128,128]{4,2,1,0,3:T(2,128)S(1)} async-done(((f32[1,1,2,128,128]{4,2,1,0,3:T(2,128)}), f32[1,1,2,128,128]{4,2,1,0,3:T(2,128)S(1)}, u32[]{:S(2)}, u32[]{:S(2)}) %all-to-all-start.3) | async-done | bytes 131104 | tf_op jit(solution)/shard_map/all_to_all | solution.py:71
  52.4 3.4 %all-to-all-start.2 = ((f32[1,1,2,128,128]{4,2,1,0,3:T(2,128)}), f32[1,1,2,128,128]{4,2,1,0,3:T(2,128)S(1)}, u32[]{:S(2)}, u32[]{:S(2)}) async-start(f32[1,1,2,128,128]{4,2,1,0,3:T(2,128)} %copy.143), calls=%async_computation.2 | async-start | bytes 262144 | tf_op jit(solution)/shard_map/all_to_all | solution.py:70
  56.7 4.5 %all-to-all-done.2 = f32[1,1,2,128,128]{4,2,1,0,3:T(2,128)S(1)} async-done(((f32[1,1,2,128,128]{4,2,1,0,3:T(2,128)}), f32[1,1,2,128,128]{4,2,1,0,3:T(2,128)S(1)}, u32[]{:S(2)}, u32[]{:S(2)}) %all-to-all-start.2) | async-done | bytes 131104 | tf_op jit(solution)/shard_map/all_to_all | solution.py:70
  66.6 3.4 %all-to-all-start.4 = ((f32[1,1,2,128,128]{3,2,1,0,4:T(2,128)}), f32[1,1,2,128,128]{3,2,1,0,4:T(2,128)S(1)}, u32[]{:S(2)}, u32[]{:S(2)}) async-start(f32[1,1,2,128,128]{3,2,1,0,4:T(2,128)} %copy.155), calls=%async_computation.4 | async-start | bytes 262144 | tf_op jit(solution)/shard_map/all_to_all | solution.py:75
  70.0 1.3 fusion.29
  72.1 3.3 %all-to-all-done.4 = f32[1,1,2,128,128]{3,2,1,0,4:T(2,128)S(1)} async-done(((f32[1,1,2,128,128]{3,2,1,0,4:T(2,128)}), f32[1,1,2,128,128]{3,2,1,0,4:T(2,128)S(1)}, u32[]{:S(2)}, u32[]{:S(2)}) %all-to-all-start.4) | async-done | bytes 131104 | tf_op jit(solution)/shard_map/all_to_all | solution.py:75
  75.4 3.4 %all-to-all-start.5 = ((f32[1,1,2,128,128]{3,2,1,0,4:T(2,128)}), f32[1,1,2,128,128]{3,2,1,0,4:T(2,128)S(1)}, u32[]{:S(2)}, u32[]{:S(2)}) async-start(f32[1,1,2,128,128]{3,2,1,0,4:T(2,128)} %copy.160), calls=%async_computation.5 | async-start | bytes 262144 | tf_op jit(solution)/shard_map/all_to_all | solution.py:76
  79.7 4.5 %all-to-all-done.5 = f32[1,1,2,128,128]{3,2,1,0,4:T(2,128)S(1)} async-done(((f32[1,1,2,128,128]{3,2,1,0,4:T(2,128)}), f32[1,1,2,128,128]{3,2,1,0,4:T(2,128)S(1)}, u32[]{:S(2)}, u32[]{:S(2)}) %all-to-all-start.5) | async-done | bytes 131104 | tf_op jit(solution)/shard_map/all_to_all | solution.py:76
  90.0 3.4 %all-to-all-start.6 = ((f32[1,1,256,128]{3,1,0,2:T(1,128)}), f32[1,1,256,128]{3,1,0,2:T(1,128)S(1)}, u32[]{:S(2)}, u32[]{:S(2)}) async-start(f32[1,1,256,128]{3,1,0,2:T(1,128)} %bitcast.822), calls=%async_computation.6 | async-start | bytes 262144 | tf_op jit(solution)/shard_map/all_to_all | solution.py:80
  93.4 1.3 fusion.23
  95.4 3.4 %all-to-all-done.6 = f32[1,1,256,128]{3,1,0,2:T(1,128)S(1)} async-done(((f32[1,1,256,128]{3,1,0,2:T(1,128)}), f32[1,1,256,128]{3,1,0,2:T(1,128)S(1)}, u32[]{:S(2)}, u32[]{:S(2)}) %all-to-all-start.6) | async-done | bytes 131104 | tf_op jit(solution)/shard_map/all_to_all | solution.py:80
  98.8 3.6 %all-to-all-start.7 = ((f32[1,1,256,128]{3,1,0,2:T(1,128)}), f32[1,1,256,128]{3,1,0,2:T(1,128)S(1)}, u32[]{:S(2)}, u32[]{:S(2)}) async-start(f32[1,1,256,128]{3,1,0,2:T(1,128)} %bitcast.823), calls=%async_computation.7 | async-start | bytes 262144 | tf_op jit(solution)/shard_map/all_to_all | solution.py:83
  103.3 4.3 %all-to-all-done.7 = f32[1,1,256,128]{3,1,0,2:T(1,128)S(1)} async-done(((f32[1,1,256,128]{3,1,0,2:T(1,128)}), f32[1,1,256,128]{3,1,0,2:T(1,128)S(1)}, u32[]{:S(2)}, u32[]{:S(2)}) %all-to-all-start.7) | async-done | bytes 131104 | tf_op jit(solution)/shard_map/all_to_all | solution.py:83
  107.9 1.2 convolution_subtract_fusion.9
  113.0 3.3 %all-to-all-start.9 = ((f32[1,1,256,128]{3,1,0,2:T(1,128)}), f32[1,1,256,128]{3,1,0,2:T(1,128)S(1)}, u32[]{:S(2)}, u32[]{:S(2)}) async-start(f32[1,1,256,128]{3,1,0,2:T(1,128)} %bitcast.824), calls=%async_computation.9 | async-start | bytes 262144 | tf_op jit(solution)/shard_map/all_to_all | solution.py:63
  116.3 1.3 fusion.21
  118.3 4.0 %all-to-all-done.9 = f32[1,1,256,128]{3,1,0,2:T(1,128)S(1)} async-done(((f32[1,1,256,128]{3,1,0,2:T(1,128)}), f32[1,1,256,128]{3,1,0,2:T(1,128)S(1)}, u32[]{:S(2)}, u32[]{:S(2)}) %all-to-all-start.9) | async-done | bytes 131104 | tf_op jit(solution)/shard_map/all_to_all | solution.py:63
  122.3 3.3 %all-to-all-start.8 = ((f32[1,1,256,128]{3,1,0,2:T(1,128)}), f32[1,1,256,128]{3,1,0,2:T(1,128)S(1)}, u32[]{:S(2)}, u32[]{:S(2)}) async-start(f32[1,1,256,128]{3,1,0,2:T(1,128)} %bitcast.825), calls=%async_computation.8 | async-start | bytes 262144 | tf_op jit(solution)/shard_map/all_to_all | solution.py:60
  126.6 5.0 %all-to-all-done.8 = f32[1,1,256,128]{3,1,0,2:T(1,128)S(1)} async-done(((f32[1,1,256,128]{3,1,0,2:T(1,128)}), f32[1,1,256,128]{3,1,0,2:T(1,128)S(1)}, u32[]{:S(2)}, u32[]{:S(2)}) %all-to-all-start.8) | async-done | bytes 131104 | tf_op jit(solution)/shard_map/all_to_all | solution.py:60
  137.0 3.4 %all-to-all-start.11 = ((f32[1,1,2,128,128]{4,2,1,0,3:T(2,128)}), f32[1,1,2,128,128]{4,2,1,0,3:T(2,128)S(1)}, u32[]{:S(2)}, u32[]{:S(2)}) async-start(f32[1,1,2,128,128]{4,2,1,0,3:T(2,128)} %copy.196), calls=%async_computation.11 | async-start | bytes 262144 | tf_op jit(solution)/shard_map/all_to_all | solution.py:71
  140.3 1.3 fusion.17
  142.5 3.3 %all-to-all-done.11 = f32[1,1,2,128,128]{4,2,1,0,3:T(2,128)S(1)} async-done(((f32[1,1,2,128,128]{4,2,1,0,3:T(2,128)}), f32[1,1,2,128,128]{4,2,1,0,3:T(2,128)S(1)}, u32[]{:S(2)}, u32[]{:S(2)}) %all-to-all-start.11) | async-done | bytes 131104 | tf_op jit(solution)/shard_map/all_to_all | solution.py:71
  145.8 3.4 %all-to-all-start.10 = ((f32[1,1,2,128,128]{4,2,1,0,3:T(2,128)}), f32[1,1,2,128,128]{4,2,1,0,3:T(2,128)S(1)}, u32[]{:S(2)}, u32[]{:S(2)}) async-start(f32[1,1,2,128,128]{4,2,1,0,3:T(2,128)} %copy.191), calls=%async_computation.10 | async-start | bytes 262144 | tf_op jit(solution)/shard_map/all_to_all | solution.py:70
  150.1 4.5 %all-to-all-done.10 = f32[1,1,2,128,128]{4,2,1,0,3:T(2,128)S(1)} async-done(((f32[1,1,2,128,128]{4,2,1,0,3:T(2,128)}), f32[1,1,2,128,128]{4,2,1,0,3:T(2,128)S(1)}, u32[]{:S(2)}, u32[]{:S(2)}) %all-to-all-start.10) | async-done | bytes 131104 | tf_op jit(solution)/shard_map/all_to_all | solution.py:70
  160.0 3.4 %all-to-all-start.12 = ((f32[1,1,2,128,128]{3,2,1,0,4:T(2,128)}), f32[1,1,2,128,128]{3,2,1,0,4:T(2,128)S(1)}, u32[]{:S(2)}, u32[]{:S(2)}) async-start(f32[1,1,2,128,128]{3,2,1,0,4:T(2,128)} %copy.203), calls=%async_computation.12 | async-start | bytes 262144 | tf_op jit(solution)/shard_map/all_to_all | solution.py:75
  163.4 1.3 fusion.11
  165.5 3.3 %all-to-all-done.12 = f32[1,1,2,128,128]{3,2,1,0,4:T(2,128)S(1)} async-done(((f32[1,1,2,128,128]{3,2,1,0,4:T(2,128)}), f32[1,1,2,128,128]{3,2,1,0,4:T(2,128)S(1)}, u32[]{:S(2)}, u32[]{:S(2)}) %all-to-all-start.12) | async-done | bytes 131104 | tf_op jit(solution)/shard_map/all_to_all | solution.py:75
  168.8 3.6 %all-to-all-start.13 = ((f32[1,1,2,128,128]{3,2,1,0,4:T(2,128)}), f32[1,1,2,128,128]{3,2,1,0,4:T(2,128)S(1)}, u32[]{:S(2)}, u32[]{:S(2)}) async-start(f32[1,1,2,128,128]{3,2,1,0,4:T(2,128)} %copy.208), calls=%async_computation.13 | async-start | bytes 262144 | tf_op jit(solution)/shard_map/all_to_all | solution.py:76
  173.3 4.3 %all-to-all-done.13 = f32[1,1,2,128,128]{3,2,1,0,4:T(2,128)S(1)} async-done(((f32[1,1,2,128,128]{3,2,1,0,4:T(2,128)}), f32[1,1,2,128,128]{3,2,1,0,4:T(2,128)S(1)}, u32[]{:S(2)}, u32[]{:S(2)}) %all-to-all-start.13) | async-done | bytes 131104 | tf_op jit(solution)/shard_map/all_to_all | solution.py:76
  183.4 3.4 %all-to-all-start.14 = ((f32[1,1,256,128]{3,1,0,2:T(1,128)}), f32[1,1,256,128]{3,1,0,2:T(1,128)S(1)}, u32[]{:S(2)}, u32[]{:S(2)}) async-start(f32[1,1,256,128]{3,1,0,2:T(1,128)} %bitcast.826), calls=%async_computation.14 | async-start | bytes 262144 | tf_op jit(solution)/shard_map/all_to_all | solution.py:80
  186.8 1.3 fusion.5
  188.8 3.4 %all-to-all-done.14 = f32[1,1,256,128]{3,1,0,2:T(1,128)S(1)} async-done(((f32[1,1,256,128]{3,1,0,2:T(1,128)}), f32[1,1,256,128]{3,1,0,2:T(1,128)S(1)}, u32[]{:S(2)}, u32[]{:S(2)}) %all-to-all-start.14) | async-done | bytes 131104 | tf_op jit(solution)/shard_map/all_to_all | solution.py:80
  192.2 3.4 %all-to-all-start.15 = ((f32[1,1,256,128]{3,1,0,2:T(1,128)}), f32[1,1,256,128]{3,1,0,2:T(1,128)S(1)}, u32[]{:S(2)}, u32[]{:S(2)}) async-start(f32[1,1,256,128]{3,1,0,2:T(1,128)} %bitcast.827), calls=%async_computation.15 | async-start | bytes 262144 | tf_op jit(solution)/shard_map/all_to_all | solution.py:83
  196.5 4.5 %all-to-all-done.15 = f32[1,1,256,128]{3,1,0,2:T(1,128)S(1)} async-done(((f32[1,1,256,128]{3,1,0,2:T(1,128)}), f32[1,1,256,128]{3,1,0,2:T(1,128)S(1)}, u32[]{:S(2)}, u32[]{:S(2)}) %all-to-all-start.15) | async-done | bytes 131104 | tf_op jit(solution)/shard_map/all_to_all | solution.py:83
  (154 shorter events, 60.9 us)
Async XLA Ops:
  0.6 15.2 %copy-start.1 = (f32[2,4,3,128,128]{4,3,2,1,0:T(8,128)S(1)}, f32[2,4,3,128,128]{4,3,2,1,0:T(8,128)}, u32[]{:S(2)}) copy-start(f32[2,4,3,128,128]{4,3,2,1,0:T(8,128)} %param.7) | copy-start | bytes 4718596
  0.6 26.1 %all-to-all-start.1 = ((f32[1,1,256,128]{3,1,0,2:T(1,128)}), f32[1,1,256,128]{3,1,0,2:T(1,128)S(1)}, u32[]{:S(2)}, u32[]{:S(2)}) async-start(f32[1,1,256,128]{3,1,0,2:T(1,128)} %bitcast.836), calls=%async_computation.1 | async-start | bytes 262144 | tf_op jit(solution)/shard_map/all_to_all | solution.py:63
  10.3 21.5 %copy-start = (f32[2,4,3,128,128]{4,3,2,1,0:T(8,128)S(1)}, f32[2,4,3,128,128]{4,3,2,1,0:T(8,128)}, u32[]{:S(2)}) copy-start(f32[2,4,3,128,128]{4,3,2,1,0:T(8,128)} %param.6) | copy-start | bytes 4718596
  26.7 11.0 %all-to-all-start = ((f32[1,1,256,128]{3,1,0,2:T(1,128)}), f32[1,1,256,128]{3,1,0,2:T(1,128)S(1)}, u32[]{:S(2)}, u32[]{:S(2)}) async-start(f32[1,1,256,128]{3,1,0,2:T(1,128)} %bitcast.837), calls=%async_computation | async-start | bytes 262144 | tf_op jit(solution)/shard_map/all_to_all | solution.py:60
  37.8 2.9 %copy-start.14 = (f32[1,1,1,128,128]{3,4,2,1,0:T(8,128)S(1)}, f32[1,1,1,128,128]{3,4,2,1,0:T(8,128)}, u32[]{:S(2)}) copy-start(f32[1,1,1,128,128]{3,4,2,1,0:T(8,128)} %copy.138) | copy-start | bytes 196612
  38.0 3.9 %copy-start.15 = (f32[1,1,1,128,128]{3,4,2,1,0:T(8,128)S(1)}, f32[1,1,1,128,128]{3,4,2,1,0:T(8,128)}, u32[]{:S(2)}) copy-start(f32[1,1,1,128,128]{3,4,2,1,0:T(8,128)} %copy.140) | copy-start | bytes 196612
  43.2 9.2 %all-to-all-start.3 = ((f32[1,1,2,128,128]{4,2,1,0,3:T(2,128)}), f32[1,1,2,128,128]{4,2,1,0,3:T(2,128)S(1)}, u32[]{:S(2)}, u32[]{:S(2)}) async-start(f32[1,1,2,128,128]{4,2,1,0,3:T(2,128)} %copy.148), calls=%async_computation.3 | async-start | bytes 262144 | tf_op jit(solution)/shard_map/all_to_all | solution.py:71
  52.4 8.8 %all-to-all-start.2 = ((f32[1,1,2,128,128]{4,2,1,0,3:T(2,128)}), f32[1,1,2,128,128]{4,2,1,0,3:T(2,128)S(1)}, u32[]{:S(2)}, u32[]{:S(2)}) async-start(f32[1,1,2,128,128]{4,2,1,0,3:T(2,128)} %copy.143), calls=%async_computation.2 | async-start | bytes 262144 | tf_op jit(solution)/shard_map/all_to_all | solution.py:70
  61.2 2.9 %copy-start.12 = (f32[1,1,1,128,128]{3,4,2,1,0:T(8,128)S(1)}, f32[1,1,1,128,128]{3,4,2,1,0:T(8,128)}, u32[]{:S(2)}) copy-start(f32[1,1,1,128,128]{3,4,2,1,0:T(8,128)} %copy.150) | copy-start | bytes 196612
  62.4 3.0 %copy-start.13 = (f32[1,1,1,128,128]{3,4,2,1,0:T(8,128)S(1)}, f32[1,1,1,128,128]{3,4,2,1,0:T(8,128)}, u32[]{:S(2)}) copy-start(f32[1,1,1,128,128]{3,4,2,1,0:T(8,128)} %copy.152) | copy-start | bytes 196612
  66.6 8.8 %all-to-all-start.4 = ((f32[1,1,2,128,128]{3,2,1,0,4:T(2,128)}), f32[1,1,2,128,128]{3,2,1,0,4:T(2,128)S(1)}, u32[]{:S(2)}, u32[]{:S(2)}) async-start(f32[1,1,2,128,128]{3,2,1,0,4:T(2,128)} %copy.155), calls=%async_computation.4 | async-start | bytes 262144 | tf_op jit(solution)/shard_map/all_to_all | solution.py:75
  75.4 8.8 %all-to-all-start.5 = ((f32[1,1,2,128,128]{3,2,1,0,4:T(2,128)}), f32[1,1,2,128,128]{3,2,1,0,4:T(2,128)S(1)}, u32[]{:S(2)}, u32[]{:S(2)}) async-start(f32[1,1,2,128,128]{3,2,1,0,4:T(2,128)} %copy.160), calls=%async_computation.5 | async-start | bytes 262144 | tf_op jit(solution)/shard_map/all_to_all | solution.py:76
  84.2 3.4 %copy-start.10 = (f32[1,1,1,128,128]{3,4,2,1,0:T(8,128)S(1)}, f32[1,1,1,128,128]{3,4,2,1,0:T(8,128)}, u32[]{:S(2)}) copy-start(f32[1,1,1,128,128]{3,4,2,1,0:T(8,128)} %copy.164) | copy-start | bytes 196612
  85.5 3.5 %copy-start.11 = (f32[1,1,1,128,128]{3,4,2,1,0:T(8,128)S(1)}, f32[1,1,1,128,128]{3,4,2,1,0:T(8,128)}, u32[]{:S(2)}) copy-start(f32[1,1,1,128,128]{3,4,2,1,0:T(8,128)} %copy.168) | copy-start | bytes 196612
  90.0 8.8 %all-to-all-start.6 = ((f32[1,1,256,128]{3,1,0,2:T(1,128)}), f32[1,1,256,128]{3,1,0,2:T(1,128)S(1)}, u32[]{:S(2)}, u32[]{:S(2)}) async-start(f32[1,1,256,128]{3,1,0,2:T(1,128)} %bitcast.822), calls=%async_computation.6 | async-start | bytes 262144 | tf_op jit(solution)/shard_map/all_to_all | solution.py:80
  98.8 8.8 %all-to-all-start.7 = ((f32[1,1,256,128]{3,1,0,2:T(1,128)}), f32[1,1,256,128]{3,1,0,2:T(1,128)S(1)}, u32[]{:S(2)}, u32[]{:S(2)}) async-start(f32[1,1,256,128]{3,1,0,2:T(1,128)} %bitcast.823), calls=%async_computation.7 | async-start | bytes 262144 | tf_op jit(solution)/shard_map/all_to_all | solution.py:83
  107.6 2.9 %copy-start.8 = (f32[1,1,1,128,128]{3,4,2,1,0:T(8,128)S(1)}, f32[1,1,1,128,128]{3,4,2,1,0:T(8,128)}, u32[]{:S(2)}) copy-start(f32[1,1,1,128,128]{3,4,2,1,0:T(8,128)} %copy.176) | copy-start | bytes 196612
  107.9 3.9 %copy-start.9 = (f32[1,1,1,128,128]{3,4,2,1,0:T(8,128)S(1)}, f32[1,1,1,128,128]{3,4,2,1,0:T(8,128)}, u32[]{:S(2)}) copy-start(f32[1,1,1,128,128]{3,4,2,1,0:T(8,128)} %copy.178) | copy-start | bytes 196612
  113.0 9.4 %all-to-all-start.9 = ((f32[1,1,256,128]{3,1,0,2:T(1,128)}), f32[1,1,256,128]{3,1,0,2:T(1,128)S(1)}, u32[]{:S(2)}, u32[]{:S(2)}) async-start(f32[1,1,256,128]{3,1,0,2:T(1,128)} %bitcast.824), calls=%async_computation.9 | async-start | bytes 262144 | tf_op jit(solution)/shard_map/all_to_all | solution.py:63
  122.3 9.2 %all-to-all-start.8 = ((f32[1,1,256,128]{3,1,0,2:T(1,128)}), f32[1,1,256,128]{3,1,0,2:T(1,128)S(1)}, u32[]{:S(2)}, u32[]{:S(2)}) async-start(f32[1,1,256,128]{3,1,0,2:T(1,128)} %bitcast.825), calls=%async_computation.8 | async-start | bytes 262144 | tf_op jit(solution)/shard_map/all_to_all | solution.py:60
  131.5 2.9 %copy-start.6 = (f32[1,1,1,128,128]{3,4,2,1,0:T(8,128)S(1)}, f32[1,1,1,128,128]{3,4,2,1,0:T(8,128)}, u32[]{:S(2)}) copy-start(f32[1,1,1,128,128]{3,4,2,1,0:T(8,128)} %copy.186) | copy-start | bytes 196612
  131.8 3.9 %copy-start.7 = (f32[1,1,1,128,128]{3,4,2,1,0:T(8,128)S(1)}, f32[1,1,1,128,128]{3,4,2,1,0:T(8,128)}, u32[]{:S(2)}) copy-start(f32[1,1,1,128,128]{3,4,2,1,0:T(8,128)} %copy.188) | copy-start | bytes 196612
  137.0 8.8 %all-to-all-start.11 = ((f32[1,1,2,128,128]{4,2,1,0,3:T(2,128)}), f32[1,1,2,128,128]{4,2,1,0,3:T(2,128)S(1)}, u32[]{:S(2)}, u32[]{:S(2)}) async-start(f32[1,1,2,128,128]{4,2,1,0,3:T(2,128)} %copy.196), calls=%async_computation.11 | async-start | bytes 262144 | tf_op jit(solution)/shard_map/all_to_all | solution.py:71
  145.8 8.8 %all-to-all-start.10 = ((f32[1,1,2,128,128]{4,2,1,0,3:T(2,128)}), f32[1,1,2,128,128]{4,2,1,0,3:T(2,128)S(1)}, u32[]{:S(2)}, u32[]{:S(2)}) async-start(f32[1,1,2,128,128]{4,2,1,0,3:T(2,128)} %copy.191), calls=%async_computation.10 | async-start | bytes 262144 | tf_op jit(solution)/shard_map/all_to_all | solution.py:70
  154.6 2.9 %copy-start.4 = (f32[1,1,1,128,128]{3,4,2,1,0:T(8,128)S(1)}, f32[1,1,1,128,128]{3,4,2,1,0:T(8,128)}, u32[]{:S(2)}) copy-start(f32[1,1,1,128,128]{3,4,2,1,0:T(8,128)} %copy.198) | copy-start | bytes 196612
  155.8 3.0 %copy-start.5 = (f32[1,1,1,128,128]{3,4,2,1,0:T(8,128)S(1)}, f32[1,1,1,128,128]{3,4,2,1,0:T(8,128)}, u32[]{:S(2)}) copy-start(f32[1,1,1,128,128]{3,4,2,1,0:T(8,128)} %copy.200) | copy-start | bytes 196612
  160.0 8.8 %all-to-all-start.12 = ((f32[1,1,2,128,128]{3,2,1,0,4:T(2,128)}), f32[1,1,2,128,128]{3,2,1,0,4:T(2,128)S(1)}, u32[]{:S(2)}, u32[]{:S(2)}) async-start(f32[1,1,2,128,128]{3,2,1,0,4:T(2,128)} %copy.203), calls=%async_computation.12 | async-start | bytes 262144 | tf_op jit(solution)/shard_map/all_to_all | solution.py:75
  168.8 8.8 %all-to-all-start.13 = ((f32[1,1,2,128,128]{3,2,1,0,4:T(2,128)}), f32[1,1,2,128,128]{3,2,1,0,4:T(2,128)S(1)}, u32[]{:S(2)}, u32[]{:S(2)}) async-start(f32[1,1,2,128,128]{3,2,1,0,4:T(2,128)} %copy.208), calls=%async_computation.13 | async-start | bytes 262144 | tf_op jit(solution)/shard_map/all_to_all | solution.py:76
  177.6 3.4 %copy-start.2 = (f32[1,1,1,128,128]{3,4,2,1,0:T(8,128)S(1)}, f32[1,1,1,128,128]{3,4,2,1,0:T(8,128)}, u32[]{:S(2)}) copy-start(f32[1,1,1,128,128]{3,4,2,1,0:T(8,128)} %copy.212) | copy-start | bytes 196612
  178.8 3.5 %copy-start.3 = (f32[1,1,1,128,128]{3,4,2,1,0:T(8,128)S(1)}, f32[1,1,1,128,128]{3,4,2,1,0:T(8,128)}, u32[]{:S(2)}) copy-start(f32[1,1,1,128,128]{3,4,2,1,0:T(8,128)} %copy.216) | copy-start | bytes 196612
  183.4 8.8 %all-to-all-start.14 = ((f32[1,1,256,128]{3,1,0,2:T(1,128)}), f32[1,1,256,128]{3,1,0,2:T(1,128)S(1)}, u32[]{:S(2)}, u32[]{:S(2)}) async-start(f32[1,1,256,128]{3,1,0,2:T(1,128)} %bitcast.826), calls=%async_computation.14 | async-start | bytes 262144 | tf_op jit(solution)/shard_map/all_to_all | solution.py:80
  192.2 8.8 %all-to-all-start.15 = ((f32[1,1,256,128]{3,1,0,2:T(1,128)}), f32[1,1,256,128]{3,1,0,2:T(1,128)S(1)}, u32[]{:S(2)}, u32[]{:S(2)}) async-start(f32[1,1,256,128]{3,1,0,2:T(1,128)} %bitcast.827), calls=%async_computation.15 | async-start | bytes 262144 | tf_op jit(solution)/shard_map/all_to_all | solution.py:83
where the time goes:
time: 209 us; the launch traced here: 207 us
  waiting for transfers between devices  60.6 us (29%)
  starting transfers between devices  59.5 us (28%)
  matrix products  52.4 us (25%)
  local copies, waits for them, and re-layouts  32.6 us (16%)
    dot_general x32, matrix products, gate_top(): jnp.einsum('...hkrl,jhk->...jrl', viewed, matrix, precision=lax.Precision...  21.2 us
    dot_general x32, matrix products, gate_low(): jnp.einsum('...l,jl->...j', x, g, precision=lax.Precision.HIGHEST, prefer...  19.3 us
    dot_general x32, matrix products, gate_mid(): jnp.einsum('...ml,jm->...jl', x, g, precision=lax.Precision.HIGHEST, pref...  11.9 us
    slice x9, local copies, waits for them, and re-layouts, on_device(): gate_imag[rnd, section, which]  10.9 us
    all_to_all x2, waiting for transfers between devices, on_device(): lax.all_to_all(merged_rows(pair[0]), 'far', split_axis=2, concat_axis=2,...  9.94 us
    all_to_all x2, starting transfers between devices, on_device(): lax.all_to_all(merged_rows(pair[1]), 'far', split_axis=2, concat_axis=2,...  9.82 us
    all_to_all x2, waiting for transfers between devices, on_device(): lax.all_to_all(pair[0], 'near', split_axis=3, concat_axis=3, tiled=True)  9 us
    all_to_all x2, waiting for transfers between devices, on_device(): lax.all_to_all(merged_rows(pair[1]), 'near', split_axis=2, concat_axis=2,...  8.82 us
  transfers between devices with their start and end apart: 16, of which 15 were waited for; matrix products, arithmetic and copies ran while one was open for 20% of the time, Pallas kernels for 0%

commit v1 on v0

--- a/solution.py
+++ b/solution.py
@@ -1,6 +1,10 @@
+import functools
+
 import jax
 import jax.numpy as jnp
 from jax import lax
+from jax.experimental import pallas as pl
+from jax.experimental.pallas import tpu as pltpu
 from jax.sharding import PartitionSpec as P
 
 
@@ -97,9 +101,226 @@
     return (real, imag)
 
 
+def dot(a, b, dims):
+    return lax.dot_general(
+        a, b, (dims, ((), ())), precision=lax.Precision.HIGHEST, preferred_element_type=jnp.float32
+    )
+
+
+def complex_matrix(greal, gimag):
+    return jnp.concatenate(
+        [jnp.concatenate([greal, -gimag], axis=1), jnp.concatenate([gimag, greal], axis=1)], axis=0
+    )
+
+
+def kernel(sizes, sr_ref, si_ref, gr_hbm, gi_hbm, or_ref, oi_ref, *scratch):
+    nfar, nnear, rounds, high, order, lows = sizes
+    sections = 4 * rounds
+    sends, recvs = scratch[: sections - 1], scratch[sections - 1 : 2 * sections - 1]
+    gr_ref, gi_ref, x_ref, send_sem, recv_sem, own_sem, gate_sem = scratch[2 * sections - 1 :]
+    far, near = lax.axis_index("far"), lax.axis_index("near")
+    upper = order // high
+    rest = order // upper
+
+    loads = [
+        pltpu.make_async_copy(gr_hbm, gr_ref, gate_sem.at[0]),
+        pltpu.make_async_copy(gi_hbm, gi_ref, gate_sem.at[1]),
+    ]
+    for load in loads:
+        load.start()
+    barrier = pltpu.get_barrier_semaphore()
+    for k in range(1, nfar):
+        pl.semaphore_signal(
+            barrier, inc=1, device_id=(lax.rem(far + k, nfar), near), device_id_type=pl.DeviceIdType.MESH
+        )
+    for k in range(1, nnear):
+        pl.semaphore_signal(
+            barrier, inc=1, device_id=(far, lax.rem(near + k, nnear)), device_id_type=pl.DeviceIdType.MESH
+        )
+    pl.semaphore_wait(barrier, nfar - 1 + nnear - 1)
+
+    pending = []
+
+    def exchange(step):
+        n, me = (nfar, far) if step % 4 == 0 else (nnear, near)
+        recv = recvs[step]
+        waits = []
+        for k in range(1, n):
+            to = lax.rem(me + k, n)
+            for c in range(2):
+                block = (sr_ref, si_ref)[c].at[to] if step == 0 else sends[step - 1].at[c, to]
+                device = (to, near) if step % 4 == 0 else (far, to)
+                copy = pltpu.make_async_remote_copy(
+                    src_ref=block,
+                    dst_ref=recv.at[c, me],
+                    send_sem=send_sem.at[step, c, k],
+                    recv_sem=recv_sem.at[step, c, k],
+                    device_id=device,
+                    device_id_type=pl.DeviceIdType.MESH,
+                )
+                copy.start()
+                pending.append(copy)
+                origin = lax.rem(me + n - k, n)
+                waits.append(
+                    pltpu.make_async_remote_copy(
+                        src_ref=recv.at[c, origin],
+                        dst_ref=recv.at[c, origin],
+                        send_sem=send_sem.at[step, c, k],
+                        recv_sem=recv_sem.at[step, c, k],
+                        device_id=device,
+                        device_id_type=pl.DeviceIdType.MESH,
+                    )
+                )
+        for c in range(2):
+            block = (sr_ref, si_ref)[c].at[me] if step == 0 else sends[step - 1].at[c, me]
+            own = pltpu.make_async_copy(block, recv.at[c, me], own_sem.at[step, c])
+            own.start()
+            own.wait()
+        if step == 0:
+            for load in loads:
+                load.wait()
+        for wait in waits:
+            wait.wait_recv()
+
+    def tops(x):
+        pieces = []
+        for c in range(2):
+            for h in range(high):
+                pieces.append(
+                    jnp.concatenate(
+                        [
+                            x[(c * rest + t) * upper : (c * rest + t + 1) * upper, h * lows : (h + 1) * lows]
+                            for t in range(rest)
+                        ],
+                        axis=1,
+                    )
+                )
+        return jnp.concatenate(pieces, axis=0)
+
+    for step in range(sections):
+        exchange(step)
+        rnd, section = step // 4, step % 4
+        recv = recvs[step]
+        low = complex_matrix(gr_ref[rnd, section, 0], gi_ref[rnd, section, 0])
+        mid = complex_matrix(
+            jnp.concatenate([gr_ref[rnd, section, 1, pl.ds(t, upper, stride=rest), :] for t in range(rest)], axis=0),
+            jnp.concatenate([gi_ref[rnd, section, 1, pl.ds(t, upper, stride=rest), :] for t in range(rest)], axis=0),
+        )
+        top = complex_matrix(gr_ref[rnd, section, 2], gi_ref[rnd, section, 2])
+        if section in (1, 2):
+            tall = jnp.concatenate(
+                [
+                    jnp.concatenate([recv[c, :, h].reshape(order, -1) for h in range(high)], axis=1)
+                    for c in range(2)
+                ],
+                axis=0,
+            )
+        else:
+            wide = jnp.concatenate([recv[c].reshape(high * order, lows) for c in range(2)], axis=1)
+        if section == 2:
+            wide = dot(low, tall, ((1,), (0,))).T
+        elif section != 1:
+            wide = dot(wide, low, ((1,), (1,)))
+        if section != 1:
+            tall = jnp.concatenate(
+                [
+                    jnp.concatenate(
+                        [wide[h * order : (h + 1) * order, c * lows : (c + 1) * lows] for h in range(high)], axis=1
+                    )
+                    for c in range(2)
+                ],
+                axis=0,
+            )
+        out = dot(top, tops(dot(mid, tall, ((1,), (0,)))), ((1,), (0,)))
+        for c in range(2):
+            for h in range(high):
+                for t in range(rest):
+                    first = (c * high + h) * upper
+                    part = out[first : first + upper, t * lows : (t + 1) * lows]
+                    if section == 1:
+                        x_ref[c, h, pl.ds(t, upper, stride=rest), :] = part
+                    elif step == sections - 1:
+                        (or_ref, oi_ref)[c][h, pl.ds(t, upper, stride=rest), :] = part
+                    elif section == 0:
+                        count = upper // nnear
+                        for b in range(nnear):
+                            sends[step][c, b, h, pl.ds(t, count, stride=rest), :] = part[
+                                b * count : (b + 1) * count
+                            ]
+                    else:
+                        n = nnear if section == 2 else nfar
+                        count = high * upper // n
+                        for i in range(n // high):
+                            sends[step][c, h * (n // high) + i, pl.ds(t, count, stride=rest), :] = part[
+                                i * count : (i + 1) * count
+                            ]
+        if section == 1:
+            wide = jnp.concatenate([x_ref[c].reshape(high * order, lows) for c in range(2)], axis=1)
+            turned = dot(low, wide, ((1,), (1,)))
+            count = lows // nnear
+            for c in range(2):
+                for h in range(high):
+                    for b in range(nnear):
+                        first = c * lows + b * count
+                        sends[step][c, b, h] = turned[first : first + count, h * order : (h + 1) * order]
+    for copy in pending:
+        copy.wait_send()
+
+
+def one_kernel(nfar, nnear, state_real, state_imag, gate_real, gate_imag):
+    shape = state_real.shape
+    high, order, lows = shape[2:]
+    rounds = gate_real.shape[0]
+    sections = 4 * rounds
+    kinds = (
+        (2, nfar, high * order // nfar, lows),
+        (2, nnear, high, order // nnear, lows),
+        (2, nnear, high, lows // nnear, order),
+        (2, nnear, high * order // nnear, lows),
+    )
+    buffers = [pltpu.VMEM(kinds[step % 4], jnp.float32) for step in range(sections)]
+    most = max(nfar, nnear)
+    vmem = pl.BlockSpec(memory_space=pltpu.VMEM)
+    anywhere = pl.BlockSpec(memory_space=pl.ANY)
+    result = jax.ShapeDtypeStruct((high, order, lows), jnp.float32)
+    real, imag = pl.pallas_call(
+        functools.partial(kernel, (nfar, nnear, rounds, high, order, lows)),
+        out_shape=(result, result),
+        in_specs=[vmem, vmem, anywhere, anywhere],
+        out_specs=(vmem, vmem),
+        scratch_shapes=buffers[1:]
+        + buffers
+        + [
+            pltpu.VMEM(gate_real.shape, jnp.float32),
+            pltpu.VMEM(gate_imag.shape, jnp.float32),
+            pltpu.VMEM((2, high, order, lows), jnp.float32),
+            pltpu.SemaphoreType.DMA((sections, 2, most)),
+            pltpu.SemaphoreType.DMA((sections, 2, most)),
+            pltpu.SemaphoreType.DMA((sections, 2)),
+            pltpu.SemaphoreType.DMA((2,)),
+        ],
+        compiler_params=pltpu.CompilerParams(collective_id=0, has_side_effects=True),
+    )(
+        state_real.reshape(kinds[0][1:]),
+        state_imag.reshape(kinds[0][1:]),
+        gate_real,
+        gate_imag,
+    )
+    return real.reshape(shape), imag.reshape(shape)
+
+
 def solution(mesh):
+    nfar, nnear = mesh.shape["far"], mesh.shape["near"]
+
+    def body(state_real, state_imag, gate_real, gate_imag):
+        high, order, lows = state_real.shape[2:]
+        tiles = (high * order // nfar, order // high // nnear, lows // nnear, high * order // nnear)
+        if any(rows < 8 or rows % 8 for rows in tiles):
+            return on_device(state_real, state_imag, gate_real, gate_imag)
+        return one_kernel(nfar, nnear, state_real, state_imag, gate_real, gate_imag)
+
     return jax.shard_map(
-        on_device,
+        body,
         mesh=mesh,
         in_specs=(P("far", "near", None, None, None), P("far", "near", None, None, None), P(), P()),
         out_specs=(P("far", "near", None, None, None), P("far", "near", None, None, None)),

time: 209 us -> 67.1 us (0.32); the launches traced: 207 us -> 66.9 us
  Pallas kernels: 0 us -> 63.1 us
  waiting for transfers between devices: 60.6 us -> 0 us
  starting transfers between devices: 59.5 us -> 0 us
  matrix products: 52.4 us -> 0 us
  local copies, waits for them, and re-layouts: 32.6 us -> 3.14 us
    pallas_call x0 -> x1, Pallas kernels: none -> 63.1 us  [one_kernel(): pl.pallas_call(functools.partial(kernel, (nfar, nnear, rounds, high, orde...]
    all_to_all x16 -> x0, waiting for transfers between devices: 60.6 us -> none  [the longest x2 9.94 us: on_device(): lax.all_to_all(merged_rows(pair[0]), 'far', split_axis=2, concat_axis=2,...]
    all_to_all x16 -> x0, starting transfers between devices: 59.5 us -> none  [the longest x2 9.82 us: on_device(): lax.all_to_all(merged_rows(pair[1]), 'far', split_axis=2, concat_axis=2,...]
    dot_general x96 -> x0, matrix products: 52.4 us -> none  [the longest x32 21.2 us: gate_top(): jnp.einsum('...hkrl,jhk->...jrl', viewed, matrix, precision=lax.Precision...]
    slice x18 -> x0, local copies, waits for them, and re-layouts: 19.6 us -> none  [the longest x9 10.9 us: on_device(): gate_imag[rnd, section, which]]
    add x12 -> x0, local copies, waits for them, and re-layouts: 6.47 us -> none  [complex_gate(): new_imag = form(imag, greal) + form(real, gimag)]
    sub x12 -> x0, local copies, waits for them, and re-layouts: 6.47 us -> none  [complex_gate(): new_real = form(real, greal) - form(imag, gimag)]
    unnamed x32 -> x2, local copies, waits for them, and re-layouts: 0.06 us -> 3.14 us
  transfers between devices with their start and end apart: 16 -> 0, of which waited for: 15 -> 0; matrix products, arithmetic and copies ran while one was open for 20% -> 0% of each run, Pallas kernels for 0% -> 0%
where the time goes in v1:
time: 67.1 us; the launch traced here: 66.9 us
  Pallas kernels  63.1 us (94%)
  local copies, waits for them, and re-layouts  3.14 us (5%)
    pallas_call x1, Pallas kernels, one_kernel(): pl.pallas_call(functools.partial(kernel, (nfar, nnear, rounds, high, orde...  63.1 us
    unnamed x2, local copies, waits for them, and re-layouts  3.14 us

profile of v1, /device:TPU:0, one launch (start us, length us, event | category | flops | bytes accessed | tf_op | source)
XLA Modules:
  0.0 66.9 jit_solution(11714785734737936311)
XLA Ops:
  0.6 63.1 %shard_map.59 = (f32[2,128,128]{2,1,0:T(8,128)}, f32[2,128,128]{2,1,0:T(8,128)}) custom-call(f32[4,64,128]{2,1,0:T(8,128)} %bitcast.6, f32[4,64,128]{2,1,0:T(8,128)} %bitcast.7, f32[2,4,3,128,128]{4,3,2,1,0:T(8,128)} %gr_hbm.1, f32[2,4,3,128,128]{4,3,2,1,0:T(8,128)} %gi_hbm.1), custom_call_target="tpu_custom_call" | custom-call | tf_op jit(solution)/shard_map/pallas_call | solution.py:286
  63.8 1.6 %copy.8 = f32[1,1,2,128,128]{4,3,2,1,0:T(8,128)} copy(f32[1,1,2,128,128]{4,3,2,1,0:T(8,128)} %bitcast.5) | data formatting | bytes 262144
  65.3 1.6 %copy.9 = f32[1,1,2,128,128]{4,3,2,1,0:T(8,128)} copy(f32[1,1,2,128,128]{4,3,2,1,0:T(8,128)} %bitcast.4) | data formatting | bytes 262144

commit v2 on v1

--- a/solution.py
+++ b/solution.py
@@ -101,10 +101,16 @@
     return (real, imag)
 
 
+def parts(x):
+    first = x.astype(jnp.bfloat16)
+    return first, (x - first.astype(jnp.float32)).astype(jnp.bfloat16)
+
+
 def dot(a, b, dims):
-    return lax.dot_general(
-        a, b, (dims, ((), ())), precision=lax.Precision.HIGHEST, preferred_element_type=jnp.float32
-    )
+    def product(x, y):
+        return lax.dot_general(x, y, (dims, ((), ())), preferred_element_type=jnp.float32)
+
+    return product(a[0], b[0]) + (product(a[0], b[1]) + product(a[1], b[0]))
 
 
 def complex_matrix(greal, gimag):
@@ -117,7 +123,7 @@
     nfar, nnear, rounds, high, order, lows = sizes
     sections = 4 * rounds
     sends, recvs = scratch[: sections - 1], scratch[sections - 1 : 2 * sections - 1]
-    gr_ref, gi_ref, x_ref, send_sem, recv_sem, own_sem, gate_sem = scratch[2 * sections - 1 :]
+    gr_ref, gi_ref, w_ref, x_ref, send_sem, recv_sem, own_sem, gate_sem = scratch[2 * sections - 1 :]
     far, near = lax.axis_index("far"), lax.axis_index("near")
     upper = order // high
     rest = order // upper
@@ -141,46 +147,51 @@
 
     pending = []
 
-    def exchange(step):
+    def launch(step, c):
         n, me = (nfar, far) if step % 4 == 0 else (nnear, near)
-        recv = recvs[step]
-        waits = []
+        source = (sr_ref, si_ref)[c] if step == 0 else sends[step - 1].at[c]
+        recv = recvs[step].at[c]
+        copies = []
         for k in range(1, n):
             to = lax.rem(me + k, n)
-            for c in range(2):
-                block = (sr_ref, si_ref)[c].at[to] if step == 0 else sends[step - 1].at[c, to]
-                device = (to, near) if step % 4 == 0 else (far, to)
-                copy = pltpu.make_async_remote_copy(
-                    src_ref=block,
-                    dst_ref=recv.at[c, me],
-                    send_sem=send_sem.at[step, c, k],
-                    recv_sem=recv_sem.at[step, c, k],
-                    device_id=device,
-                    device_id_type=pl.DeviceIdType.MESH,
-                )
-                copy.start()
-                pending.append(copy)
-                origin = lax.rem(me + n - k, n)
-                waits.append(
-                    pltpu.make_async_remote_copy(
-                        src_ref=recv.at[c, origin],
-                        dst_ref=recv.at[c, origin],
-                        send_sem=send_sem.at[step, c, k],
-                        recv_sem=recv_sem.at[step, c, k],
-                        device_id=device,
-                        device_id_type=pl.DeviceIdType.MESH,
-                    )
-                )
-        for c in range(2):
-            block = (sr_ref, si_ref)[c].at[me] if step == 0 else sends[step - 1].at[c, me]
-            own = pltpu.make_async_copy(block, recv.at[c, me], own_sem.at[step, c])
-            own.start()
-            own.wait()
-        if step == 0:
-            for load in loads:
-                load.wait()
-        for wait in waits:
-            wait.wait_recv()
+            copy = pltpu.make_async_remote_copy(
+                src_ref=source.at[to],
+                dst_ref=recv.at[me],
+                send_sem=send_sem.at[step, c, k],
+                recv_sem=recv_sem.at[step, c, k],
+                device_id=(to, near) if step % 4 == 0 else (far, to),
+                device_id_type=pl.DeviceIdType.MESH,
+            )
+            copy.start()
+            pending.append(copy)
+        own = pltpu.make_async_copy(source.at[me], recv.at[me], own_sem.at[step, c])
+        own.start()
+
+    def arrive(step, c):
+        n, me = (nfar, far) if step % 4 == 0 else (nnear, near)
+        recv = recvs[step].at[c]
+        pltpu.make_async_copy(recv.at[me], recv.at[me], own_sem.at[step, c]).wait()
+        for k in range(1, n):
+            origin = lax.rem(me + n - k, n)
+            pltpu.make_async_remote_copy(
+                src_ref=recv.at[origin],
+                dst_ref=recv.at[origin],
+                send_sem=send_sem.at[step, c, k],
+                recv_sem=recv_sem.at[step, c, k],
+                device_id=(origin, near) if step % 4 == 0 else (far, origin),
+                device_id_type=pl.DeviceIdType.MESH,
+            ).wait_recv()
+
+    def put(which, matrix):
+        w_ref[which, 0], w_ref[which, 1] = parts(matrix)
+
+    def get(which, rows, columns):
+        return w_ref[which, 0, rows, columns], w_ref[which, 1, rows, columns]
+
+    every = slice(None)
+
+    def half(c):
+        return slice(c * order, (c + 1) * order)
 
     def tops(x):
         pieces = []
@@ -197,31 +208,39 @@
                 )
         return jnp.concatenate(pieces, axis=0)
 
+    for c in range(2):
+        launch(0, c)
+    for load in loads:
+        load.wait()
     for step in range(sections):
-        exchange(step)
         rnd, section = step // 4, step % 4
         recv = recvs[step]
         low = complex_matrix(gr_ref[rnd, section, 0], gi_ref[rnd, section, 0])
-        mid = complex_matrix(
-            jnp.concatenate([gr_ref[rnd, section, 1, pl.ds(t, upper, stride=rest), :] for t in range(rest)], axis=0),
-            jnp.concatenate([gi_ref[rnd, section, 1, pl.ds(t, upper, stride=rest), :] for t in range(rest)], axis=0),
+        put(0, low.T if section in (0, 3) else low)
+        put(
+            1,
+            complex_matrix(
+                jnp.concatenate(
+                    [gr_ref[rnd, section, 1, pl.ds(t, upper, stride=rest), :] for t in range(rest)], axis=0
+                ),
+                jnp.concatenate(
+                    [gi_ref[rnd, section, 1, pl.ds(t, upper, stride=rest), :] for t in range(rest)], axis=0
+                ),
+            ),
         )
-        top = complex_matrix(gr_ref[rnd, section, 2], gi_ref[rnd, section, 2])
-        if section in (1, 2):
-            tall = jnp.concatenate(
-                [
-                    jnp.concatenate([recv[c, :, h].reshape(order, -1) for h in range(high)], axis=1)
-                    for c in range(2)
-                ],
-                axis=0,
-            )
-        else:
-            wide = jnp.concatenate([recv[c].reshape(high * order, lows) for c in range(2)], axis=1)
-        if section == 2:
-            wide = dot(low, tall, ((1,), (0,))).T
-        elif section != 1:
-            wide = dot(wide, low, ((1,), (1,)))
+        put(2, complex_matrix(gr_ref[rnd, section, 2], gi_ref[rnd, section, 2]))
+        begun = []
+        for c in range(2):
+            arrive(step, c)
+            if section in (1, 2):
+                tall = jnp.concatenate([recv[c, :, h].reshape(order, -1) for h in range(high)], axis=1)
+                begun.append(dot(get(2 - section, every, half(c)), parts(tall), ((1,), (0,))))
+            else:
+                wide = recv[c].reshape(high * order, lows)
+                begun.append(dot(parts(wide), get(0, half(c), every), ((1,), (0,))))
+        state = begun[0] + begun[1]
         if section != 1:
+            wide = state.T if section == 2 else state
             tall = jnp.concatenate(
                 [
                     jnp.concatenate(
@@ -231,12 +250,13 @@
                 ],
                 axis=0,
             )
-        out = dot(top, tops(dot(mid, tall, ((1,), (0,)))), ((1,), (0,)))
+            state = dot(get(1, every, every), parts(tall), ((1,), (0,)))
+        ready = parts(tops(state))
         for c in range(2):
+            out = dot(get(2, half(c), every), ready, ((1,), (0,)))
             for h in range(high):
                 for t in range(rest):
-                    first = (c * high + h) * upper
-                    part = out[first : first + upper, t * lows : (t + 1) * lows]
+                    part = out[h * upper : (h + 1) * upper, t * lows : (t + 1) * lows]
                     if section == 1:
                         x_ref[c, h, pl.ds(t, upper, stride=rest), :] = part
                     elif step == sections - 1:
@@ -254,15 +274,17 @@
                             sends[step][c, h * (n // high) + i, pl.ds(t, count, stride=rest), :] = part[
                                 i * count : (i + 1) * count
                             ]
+            if section != 1 and step < sections - 1:
+                launch(step + 1, c)
         if section == 1:
-            wide = jnp.concatenate([x_ref[c].reshape(high * order, lows) for c in range(2)], axis=1)
-            turned = dot(low, wide, ((1,), (1,)))
+            wide = parts(jnp.concatenate([x_ref[c].reshape(high * order, lows) for c in range(2)], axis=1))
             count = lows // nnear
             for c in range(2):
+                turned = dot(get(0, half(c), every), wide, ((1,), (1,)))
                 for h in range(high):
                     for b in range(nnear):
-                        first = c * lows + b * count
-                        sends[step][c, b, h] = turned[first : first + count, h * order : (h + 1) * order]
+                        sends[step][c, b, h] = turned[b * count : (b + 1) * count, h * order : (h + 1) * order]
+                launch(step + 1, c)
     for copy in pending:
         copy.wait_send()
 
@@ -293,6 +315,7 @@
         + [
             pltpu.VMEM(gate_real.shape, jnp.float32),
             pltpu.VMEM(gate_imag.shape, jnp.float32),
+            pltpu.VMEM((3, 2, 2 * order, 2 * order), jnp.bfloat16),
             pltpu.VMEM((2, high, order, lows), jnp.float32),
             pltpu.SemaphoreType.DMA((sections, 2, most)),
             pltpu.SemaphoreType.DMA((sections, 2, most)),

time: 67.1 us -> 62.9 us (0.937)
  Pallas kernels: 63.1 us -> 59 us
    pallas_call x1, Pallas kernels: 63.1 us -> 59 us  [one_kernel(): pl.pallas_call(functools.partial(kernel, (nfar, nnear, rounds, high, orde...]
where the time goes in v2:
time: 62.9 us; the launch traced here: 62.8 us
  Pallas kernels  59 us (94%)
  local copies, waits for them, and re-layouts  3.14 us (5%)
  between operations  0.64 us (1%)
    pallas_call x1, Pallas kernels, one_kernel(): pl.pallas_call(functools.partial(kernel, (nfar, nnear, rounds, high, orde...  59 us
    unnamed x2, local copies, waits for them, and re-layouts  3.14 us

profile of v2, /device:TPU:0, one launch (start us, length us, event | category | flops | bytes accessed | tf_op | source)
XLA Modules:
  0.0 62.8 jit_solution(1542237305250031508)
XLA Ops:
  0.6 59.0 %shard_map.59 = (f32[2,128,128]{2,1,0:T(8,128)}, f32[2,128,128]{2,1,0:T(8,128)}) custom-call(f32[4,64,128]{2,1,0:T(8,128)} %bitcast.6, f32[4,64,128]{2,1,0:T(8,128)} %bitcast.7, f32[2,4,3,128,128]{4,3,2,1,0:T(8,128)} %gr_hbm.1, f32[2,4,3,128,128]{4,3,2,1,0:T(8,128)} %gi_hbm.1), custom_call_target="tpu_custom_call" | custom-call | tf_op jit(solution)/shard_map/pallas_call | solution.py:308
  59.6 1.6 %copy.8 = f32[1,1,2,128,128]{4,3,2,1,0:T(8,128)} copy(f32[1,1,2,128,128]{4,3,2,1,0:T(8,128)} %bitcast.5) | data formatting | bytes 262144
  61.2 1.6 %copy.9 = f32[1,1,2,128,128]{4,3,2,1,0:T(8,128)} copy(f32[1,1,2,128,128]{4,3,2,1,0:T(8,128)} %bitcast.4) | data formatting | bytes 262144

commit v3 on v2

--- a/solution.py
+++ b/solution.py
@@ -304,7 +304,7 @@
     most = max(nfar, nnear)
     vmem = pl.BlockSpec(memory_space=pltpu.VMEM)
     anywhere = pl.BlockSpec(memory_space=pl.ANY)
-    result = jax.ShapeDtypeStruct((high, order, lows), jnp.float32)
+    result = pltpu.VMEM((high, order, lows), jnp.float32)
     real, imag = pl.pallas_call(
         functools.partial(kernel, (nfar, nnear, rounds, high, order, lows)),
         out_shape=(result, result),

time: 62.9 us -> 60.4 us (0.960)
  local copies, waits for them, and re-layouts: 3.14 us -> 1.31 us
  Pallas kernels: 59 us -> 58.3 us
    unnamed x2, local copies, waits for them, and re-layouts: 3.14 us -> 1.31 us
    pallas_call x1, Pallas kernels: 59 us -> 58.3 us  [one_kernel(): pl.pallas_call(functools.partial(kernel, (nfar, nnear, rounds, high, orde...]
where the time goes in v3:
time: 60.4 us; the launch traced here: 60.3 us
  Pallas kernels  58.3 us (97%)
  local copies, waits for them, and re-layouts  1.31 us (2%)
  between operations  0.64 us (1%)
    pallas_call x1, Pallas kernels, one_kernel(): pl.pallas_call(functools.partial(kernel, (nfar, nnear, rounds, high, orde...  58.3 us
    unnamed x2, local copies, waits for them, and re-layouts  1.31 us

profile of v3, /device:TPU:0, one launch (start us, length us, event | category | flops | bytes accessed | tf_op | source)
XLA Modules:
  0.0 60.3 jit_solution(14168383639090815981)
XLA Ops:
  0.6 58.3 %shard_map.59 = (f32[2,128,128]{2,1,0:T(8,128)S(1)}, f32[2,128,128]{2,1,0:T(8,128)S(1)}) custom-call(f32[4,64,128]{2,1,0:T(8,128)} %bitcast.6, f32[4,64,128]{2,1,0:T(8,128)} %bitcast.7, f32[2,4,3,128,128]{4,3,2,1,0:T(8,128)} %gr_hbm.1, f32[2,4,3,128,128]{4,3,2,1,0:T(8,128)} %gi_hbm.1), custom_call_target="tpu_custom_call" | custom-call | tf_op jit(solution)/shard_map/pallas_call | solution.py:308
  58.9 0.7 %copy.8 = f32[1,1,2,128,128]{4,3,2,1,0:T(8,128)} copy(f32[1,1,2,128,128]{4,3,2,1,0:T(8,128)S(1)} %bitcast.5) | data formatting | bytes 262144
  59.6 0.7 %copy.9 = f32[1,1,2,128,128]{4,3,2,1,0:T(8,128)} copy(f32[1,1,2,128,128]{4,3,2,1,0:T(8,128)S(1)} %bitcast.4) | data formatting | bytes 262144
